TPU v7x, 32 devices: a whole 2x2x4 slice. The times are simulated.
32 devices in a mesh: items: 8 (over y, x, core), heads: 4 (over z).
Axes of the slice: x: 2, y: 2, z: 4, core: 2. Of those that a mesh axis runs over, the one named last changes fastest.
Arguments:
- tokens: bfloat16 [16, 1280, 768], P('items', 'heads'), may hold values from -6 to 6
- passes: int32 [16], P('items'), may hold values from 2 to 5, as said below
- embed: bfloat16 [5, 768], replicated, may hold values from -3 to 3
- gain_one: bfloat16 [768], replicated, may hold values from 0.5 to 1.5
- w_qkv: bfloat16 [768, 2304], replicated, may hold values from -0.3125 to 0.3125
- w_out: bfloat16 [768, 768], replicated, may hold values from -2 to 2
- gain_two: bfloat16 [768], replicated, may hold values from 0.5 to 1.5
- w_up: bfloat16 [768, 3072], replicated, may hold values from -0.21875 to 0.21875
- w_down: bfloat16 [3072, 768], replicated, may hold values from -0.109375 to 0.109375
- cotangent: bfloat16 [16, 1280, 768], P('items', 'heads'), may hold values from -6 to 6
Outputs:
- outputs: bfloat16 [16, 1280, 768], P('items', 'heads')
- grad_tokens: bfloat16 [16, 1280, 768], P('items', 'heads')
- grad_embed: float32 [5, 768], P(None, 'heads')
- grad_gain_one: float32 [768], P('heads')
- grad_w_qkv: float32 [768, 2304], P('heads')
- grad_w_out: float32 [768, 768], P('heads')
- grad_gain_two: float32 [768], P('heads')
- grad_w_up: float32 [768, 3072], P('heads')
- grad_w_down: float32 [3072, 768], P('heads')
Inputs may be any that keep to these rules, and one draw needn't show every extreme that they name: Each item's number of passes; every draw holds an item with 2 passes and one with 5.
All inputs are finite; a program needn't handle non-finite values.
Results may differ from a plain program's by a relative error of at most 0.013.
Values may be sent and summed in bfloat16 or wider, within the bound.
A program may use at most 192 MiB of HBM per device.

v0:
```python
import jax
import jax.numpy as jnp
from jax import lax
from jax.sharding import PartitionSpec as P

HEADS = 12
HEAD_DIM = 64
PASSES_MAX = 5
TOK_PASS = 256


highest = lax.Precision.HIGHEST
epsilon = 1e-05
masked_fill = -1e30


def layer_norm(values_in, gain):
    centered = values_in - jnp.mean(values_in, axis=-1, keepdims=True)
    spread = jnp.mean(centered * centered, axis=-1, keepdims=True)
    return centered * lax.rsqrt(spread + epsilon) * gain


def gelu_tanh(values_in):
    return jax.nn.gelu(values_in, approximate=True)


def masked_scores(queries, keys_in, query_slots, key_slots, valid_len):
    scores = jnp.einsum(
        "qhd,khd->hqk", queries, keys_in, preferred_element_type=jnp.float32
    ) * HEAD_DIM ** (-0.5)
    allowed = (key_slots[None, :] <= query_slots[:, None]) & (key_slots[None, :] < valid_len)
    return jnp.where(allowed[None], scores, masked_fill)


def attend(queries, keys_in, values_in, query_slots, key_slots, valid_len):
    masked = masked_scores(queries, keys_in, query_slots, key_slots, valid_len)
    row_max = jnp.max(masked, axis=-1, keepdims=True)
    exp_scores = jnp.exp(masked - row_max)
    row_total = jnp.sum(exp_scores, axis=-1, keepdims=True)
    prob_low = (exp_scores / row_total).astype(jnp.bfloat16)
    mixed_out = jnp.einsum("hqk,khd->qhd", prob_low, values_in, preferred_element_type=jnp.float32)
    return (mixed_out.astype(jnp.bfloat16), row_max + jnp.log(row_total))


def attend_back(
    queries, keys_in, values_in, grad_mixed, query_slots, key_slots, valid_len, log_total
):
    masked = masked_scores(queries, keys_in, query_slots, key_slots, valid_len)
    prob_full = jnp.exp(masked - log_total)
    prob_low = prob_full.astype(jnp.bfloat16)
    grad_values = jnp.einsum(
        "hqk,qhd->khd", prob_low, grad_mixed, preferred_element_type=jnp.float32
    )
    grad_probs = jnp.einsum(
        "qhd,khd->hqk", grad_mixed, values_in, preferred_element_type=jnp.float32
    )
    row_inner = jnp.sum(grad_probs * prob_full, axis=-1, keepdims=True)
    grad_scores = (prob_full * (grad_probs - row_inner)).astype(jnp.bfloat16)
    grad_queries = jnp.einsum(
        "hqk,khd->qhd", grad_scores, keys_in, preferred_element_type=jnp.float32
    ) * HEAD_DIM ** (-0.5)
    grad_keys = jnp.einsum(
        "hqk,qhd->khd", grad_scores, queries, preferred_element_type=jnp.float32
    ) * HEAD_DIM ** (-0.5)
    return (grad_queries, grad_keys, grad_values)


def on_device(tokens, passes, embed, gain_one, w_qkv, w_out, gain_two, w_up, w_down, cotangent):
    groups = lax.axis_size("heads")
    item_count, span_here, model_width = tokens.shape
    row_count = item_count * span_here
    full_len = span_here * groups
    slot_index = lax.axis_index("heads") * span_here + jnp.arange(span_here, dtype=jnp.int32)
    whole_slots = jnp.arange(full_len, dtype=jnp.int32)
    valid_len = TOK_PASS * passes
    is_valid = (slot_index[None, :] < valid_len[:, None]).astype(jnp.float32)
    pass_index = slot_index[None, :] % passes[:, None]
    onehot = (
        pass_index[:, :, None] == jnp.arange(PASSES_MAX, dtype=jnp.int32)[None, None, :]
    ).astype(jnp.float32)
    hidden = tokens.astype(jnp.float32) + jnp.einsum(
        "ilk,kd->ild", onehot, embed.astype(jnp.float32), precision=highest
    )
    hidden = hidden.reshape(row_count, model_width)
    normed, norm_one_back = jax.vjp(layer_norm, hidden, gain_one.astype(jnp.float32))
    normed_low = normed.astype(jnp.bfloat16)
    qkv_rows = jnp.dot(normed_low, w_qkv, preferred_element_type=jnp.float32).astype(jnp.bfloat16)
    shaped = qkv_rows.reshape(item_count, span_here, 3, HEADS, HEAD_DIM)
    queries, keys_local, values_local = (shaped[:, :, 0], shaped[:, :, 1], shaped[:, :, 2])
    head_q, head_k, head_v = (
        lax.all_to_all(queries, "heads", split_axis=2, concat_axis=1, tiled=True),
        lax.all_to_all(keys_local, "heads", split_axis=2, concat_axis=1, tiled=True),
        lax.all_to_all(values_local, "heads", split_axis=2, concat_axis=1, tiled=True),
    )

    def attend_item(inputs):
        item_q, item_k, item_v, item_len = inputs
        return attend(item_q, item_k, item_v, whole_slots, whole_slots, item_len)

    head_mixed, log_totals = lax.map(attend_item, (head_q, head_k, head_v, valid_len))
    mixed_out = lax.all_to_all(head_mixed, "heads", split_axis=1, concat_axis=2, tiled=True)
    mixed_rows = mixed_out.reshape(row_count, model_width)
    middle = hidden + jnp.dot(mixed_rows, w_out, preferred_element_type=jnp.float32)
    second, norm_two_back = jax.vjp(layer_norm, middle, gain_two.astype(jnp.float32))
    second_low = second.astype(jnp.bfloat16)
    up_proj = jnp.dot(second_low, w_up, preferred_element_type=jnp.float32)
    active, gelu_back = jax.vjp(gelu_tanh, up_proj)
    active_low = active.astype(jnp.bfloat16)
    result = middle + jnp.dot(active_low, w_down, preferred_element_type=jnp.float32)
    row_mask = is_valid.reshape(row_count, 1)
    outputs = (result * row_mask).astype(jnp.bfloat16).reshape(item_count, span_here, model_width)
    grad_result = cotangent.astype(jnp.float32).reshape(row_count, model_width) * row_mask
    grad_low = grad_result.astype(jnp.bfloat16)
    grad_w_down = jnp.dot(active_low.T, grad_low, preferred_element_type=jnp.float32)
    (grad_up,) = gelu_back(jnp.dot(grad_low, w_down.T, preferred_element_type=jnp.float32))
    grad_up_low = grad_up.astype(jnp.bfloat16)
    grad_w_up = jnp.dot(second_low.T, grad_up_low, preferred_element_type=jnp.float32)
    grad_middle_norm, grad_gain_two = norm_two_back(
        jnp.dot(grad_up_low, w_up.T, preferred_element_type=jnp.float32)
    )
    grad_middle = grad_result + grad_middle_norm
    grad_branch = grad_middle.astype(jnp.bfloat16)
    grad_w_out = jnp.dot(mixed_rows.T, grad_branch, preferred_element_type=jnp.float32)
    grad_mixed = jnp.dot(grad_branch, w_out.T, preferred_element_type=jnp.float32).astype(
        jnp.bfloat16
    )
    grad_mixed = grad_mixed.reshape(item_count, span_here, HEADS, HEAD_DIM)
    head_grad = lax.all_to_all(grad_mixed, "heads", split_axis=2, concat_axis=1, tiled=True)

    def back_item(inputs):
        item_q, item_k, item_v, item_grad, item_lse, item_len = inputs
        pieces = attend_back(
            item_q, item_k, item_v, item_grad, whole_slots, whole_slots, item_len, item_lse
        )
        return tuple((piece.astype(jnp.bfloat16) for piece in pieces))

    grad_hq, grad_hk, grad_hv = lax.map(
        back_item, (head_q, head_k, head_v, head_grad, log_totals, valid_len)
    )
    grad_q, grad_k, grad_v = (
        lax.all_to_all(grad_hq, "heads", split_axis=1, concat_axis=2, tiled=True),
        lax.all_to_all(grad_hk, "heads", split_axis=1, concat_axis=2, tiled=True),
        lax.all_to_all(grad_hv, "heads", split_axis=1, concat_axis=2, tiled=True),
    )
    grad_qkv = jnp.stack((grad_q, grad_k, grad_v), axis=2).reshape(row_count, 3 * model_width)
    grad_w_qkv = jnp.dot(normed_low.T, grad_qkv, preferred_element_type=jnp.float32)
    grad_hidden_norm, grad_gain_one = norm_one_back(
        jnp.dot(grad_qkv, w_qkv.T, preferred_element_type=jnp.float32)
    )
    grad_hidden = grad_middle + grad_hidden_norm
    grad_tokens = grad_hidden.astype(jnp.bfloat16).reshape(item_count, span_here, model_width)
    grad_embed = jnp.einsum(
        "ilk,ild->kd",
        onehot,
        grad_hidden.reshape(item_count, span_here, model_width),
        precision=highest,
    )
    shares = (
        lax.psum_scatter(grad_embed, "heads", scatter_dimension=1, tiled=True),
        lax.psum_scatter(grad_gain_one, "heads", scatter_dimension=0, tiled=True),
        lax.psum_scatter(grad_w_qkv, "heads", scatter_dimension=0, tiled=True),
        lax.psum_scatter(grad_w_out, "heads", scatter_dimension=0, tiled=True),
        lax.psum_scatter(grad_gain_two, "heads", scatter_dimension=0, tiled=True),
        lax.psum_scatter(grad_w_up, "heads", scatter_dimension=0, tiled=True),
        lax.psum_scatter(grad_w_down, "heads", scatter_dimension=0, tiled=True),
    )
    embed_total, gain_one_total, qkv_total, out_total, gain_two_total, up_total, down_total = (
        lax.psum(
            (shares[0], shares[1], shares[2], shares[3], shares[4], shares[5], shares[6]), "items"
        )
    )
    return (
        outputs,
        grad_tokens,
        embed_total,
        gain_one_total,
        qkv_total,
        out_total,
        gain_two_total,
        up_total,
        down_total,
    )


def solution(mesh):
    return jax.shard_map(
        on_device,
        mesh=mesh,
        in_specs=(
            P("items", "heads", None),
            P("items"),
            P(),
            P(),
            P(),
            P(),
            P(),
            P(),
            P(),
            P("items", "heads", None),
        ),
        out_specs=(
            P("items", "heads", None),
            P("items", "heads", None),
            P(None, "heads"),
            P("heads"),
            P("heads", None),
            P("heads", None),
            P("heads"),
            P("heads", None),
            P("heads", None),
        ),
        check_vma=False,
    )
```

profile of v0, /device:TPU:0, one launch (start us, length us, event | category | flops | bytes accessed | tf_op | source)
XLA Modules:
  0.0 1243.3 jit_solution(1967537181882224964)
XLA Ops:
  19.1 4.1 convolution_convert_fusion
  23.2 5.4 copy.88
  28.6 8.3 reshape.347
  36.9 4.7 slice_bitcast_fusion
  41.5 34.8 %all_to_all.132 = bf16[2,320,12,64]{1,0,3,2:T(2,128)(2,1)} all-to-all(bf16[2,320,12,64]{1,0,3,2:T(2,128)(2,1)S(1)} %get-tuple-element.263), channel_id=1, replica_groups=mesh['items'=8,'heads'=4] {'heads'}, dimensions={2} | all-to-all | bytes 1966080 | tf_op jit(solution)/shard_map/all_to_all | solution.py:92
  76.3 30.9 %all_to_all.133 = bf16[2,320,12,64]{1,0,3,2:T(2,128)(2,1)} all-to-all(bf16[2,320,12,64]{1,0,3,2:T(2,128)(2,1)S(1)} %get-tuple-element.264), channel_id=1, replica_groups=mesh['items'=8,'heads'=4] {'heads'}, dimensions={2} | all-to-all | bytes 1966080 | tf_op jit(solution)/shard_map/all_to_all | solution.py:91
  107.2 4.3 all-to-all-start
  124.0 15.1 %all-to-all-done = bf16[2,320,12,64]{1,0,3,2:T(2,128)(2,1)} async-done(((bf16[2,320,12,64]{1,0,3,2:T(2,128)(2,1)}), bf16[2,320,12,64]{1,0,3,2:T(2,128)(2,1)}, u32[]{:S(2)}, u32[]{:S(2)}) %all-to-all-start) | async-done | bytes 983072 | tf_op jit(solution)/shard_map/all_to_all | solution.py:93
  146.4 73.3 %while.30 = (s32[]{:T(128)}, bf16[2,1280,3,64]{1,3,2,0:T(8,128)(2,1)}, f32[2,3,1280,1]{2,1,3,0:T(4,128)}, bf16[2,1280,3,64]{1,3,2,0:T(8,128)(2,1)}, s32[2]{0:T(1...) while((s32[]{:T(128)}, ...), condition=%wide.region_5.6_spmd.clone.clone, body=%wide.region_2.5_spmd.clone.clone.sunk | while | flops 1301132800 | bytes 64747232 | solution.py:100
  149.6 12.2 fusion.121
  161.8 9.8 fusion.122
  171.6 11.0 fusion.123
  186.1 12.2 fusion.121
  198.3 9.8 fusion.122
  208.1 10.9 fusion.123
  219.7 5.0 copy.95
  224.7 4.3 reshape.365
  229.0 15.2 %all-to-all-start.3 = ((bf16[4,2,61440]{2,1,0:T(2,128)(2,1)}), bf16[4,2,61440]{2,1,0:T(2,128)(2,1)}, u32[]{:S(2)}, u32[]{:S(2)}) async-start(bf16[4,2,61440]{2,1,0:T(2,128)(2,1)} %reshape.365), calls=%async_computation.3 | async-start | bytes 1966080 | tf_op jit(solution)/shard_map/all_to_all | solution.py:101
  246.8 7.8 fusion.76
  254.5 13.3 %all-to-all-done.3 = bf16[4,2,61440]{2,1,0:T(2,128)(2,1)} async-done(((bf16[4,2,61440]{2,1,0:T(2,128)(2,1)}), bf16[4,2,61440]{2,1,0:T(2,128)(2,1)}, u32[]{:S(2)}, u32[]{:S(2)}) %all-to-all-start.3) | async-done | bytes 983072 | tf_op jit(solution)/shard_map/all_to_all | solution.py:101
  267.9 4.2 reshape.366
  272.1 6.7 copy.96
  286.9 12.0 fusion.58
  299.0 4.1 multiply_reduce_fusion.1
  314.5 31.6 %all_to_all.134 = bf16[2,320,12,64]{1,0,3,2:T(2,128)(2,1)S(1)} all-to-all(bf16[2,320,12,64]{1,0,3,2:T(2,128)(2,1)} %reshape.352), channel_id=1, replica_groups=mesh['items'=8,'heads'=4] {'heads'}, dimensions={2} | all-to-all | bytes 1966080 | tf_op jit(solution)/shard_map/all_to_all | solution.py:128
  354.2 116.2 %while.31 = (s32[]{:T(128)}, bf16[2,1280,3,64]{1,3,2,0:T(8,128)(2,1)}, bf16[2,1280,3,64]{1,3,2,0:T(8,128)(2,1)}, bf16[2,1280,3,64]{1,3,2,0:T(8,128)(2,1)}, bf16[...) while((s32[]{:T(128)}, ...), condition=%wide.region_12.13_spmd.clone.clone, body=%wide.region_10.12_spmd.clone.clone.sunk | while | flops 3194467840 | bytes 195054544 | solution.py:137
  358.2 11.7 fusion.132
  370.0 9.9 fusion.135
  379.9 12.7 %multiply_reduce_fusion.8 = (f32[3,1280]{1,0:T(4,128)S(1)}, f32[3,1280,1280]{1,2,0:T(8,128)}) fusion(f32[3,1280,1280]{1,2,0:T(8,128)} %fusion.132, bf16[2,1280,3,64]{1,3,2,0:T(8,128)(2,1)S(1)} %copy-done.8, s32[]{:T(128)S(6)} %copy.137, bf16[2,1280,3,64]{1,3,2,0:T(8,128)(2,1)S(1)} %copy-done.2), kind=kOutput, calls=%fused_computation.27.clone.1 | convolution fusion | flops 638972160 | bytes 40321024 | tf_op jit(solution)/shard_map/while/body/eval_jaxpr/qhd,khd->hqk/dot_general | solution.py:54
  392.6 13.8 %multiply_convert_fusion.11 = bf16[3,1280,1280]{1,2,0:T(8,128)(2,1)S(1)} fusion(f32[3,1280,1280]{1,2,0:T(8,128)} %get-tuple-element.388, f32[3,1280,1280]{1,2,0:T(8,128)} %fusion.132, f32[3,1280]{1,0:T(4,128)S(1)} %get-tuple-element.389), kind=kLoop, calls=%fused_computation.26.clone.1 | loop fusion | flops 14745600 | bytes 49167360 | tf_op jit(solution)/shard_map/while/body/eval_jaxpr/convert_element_type | solution.py:58
  416.1 11.7 fusion.132
  427.8 9.9 fusion.135
  437.7 12.7 %multiply_reduce_fusion.8 = (f32[3,1280]{1,0:T(4,128)S(1)}, f32[3,1280,1280]{1,2,0:T(8,128)}) fusion(f32[3,1280,1280]{1,2,0:T(8,128)} %fusion.132, bf16[2,1280,3,64]{1,3,2,0:T(8,128)(2,1)S(1)} %copy-done.8, s32[]{:T(128)S(6)} %copy.137, bf16[2,1280,3,64]{1,3,2,0:T(8,128)(2,1)S(1)} %copy-done.2), kind=kOutput, calls=%fused_computation.27.clone.1 | convolution fusion | flops 638972160 | bytes 40321024 | tf_op jit(solution)/shard_map/while/body/eval_jaxpr/qhd,khd->hqk/dot_general | solution.py:54
  450.4 13.8 %multiply_convert_fusion.11 = bf16[3,1280,1280]{1,2,0:T(8,128)(2,1)S(1)} fusion(f32[3,1280,1280]{1,2,0:T(8,128)} %get-tuple-element.388, f32[3,1280,1280]{1,2,0:T(8,128)} %fusion.132, f32[3,1280]{1,0:T(4,128)S(1)} %get-tuple-element.389), kind=kLoop, calls=%fused_computation.26.clone.1 | loop fusion | flops 14745600 | bytes 49167360 | tf_op jit(solution)/shard_map/while/body/eval_jaxpr/convert_element_type | solution.py:58
  470.4 5.0 copy.106
  475.4 4.3 reshape.367
  479.7 4.2 all-to-all-start.7
  488.0 5.1 copy.100
  493.1 4.4 reshape.371
  497.4 27.0 %all-to-all-done.7 = bf16[4,2,61440]{2,1,0:T(2,128)(2,1)} async-done(((bf16[4,2,61440]{2,1,0:T(2,128)(2,1)}), bf16[4,2,61440]{2,1,0:T(2,128)(2,1)}, u32[]{:S(2)}, u32[]{:S(2)}) %all-to-all-start.7) | async-done | bytes 983072 | tf_op jit(solution)/shard_map/all_to_all | solution.py:143
  524.5 6.1 all-to-all-start.5
  530.6 5.1 copy.103
  535.7 4.3 reshape.369
  540.0 26.3 %all-to-all-done.5 = bf16[4,2,61440]{2,1,0:T(2,128)(2,1)} async-done(((bf16[4,2,61440]{2,1,0:T(2,128)(2,1)}), bf16[4,2,61440]{2,1,0:T(2,128)(2,1)}, u32[]{:S(2)}, u32[]{:S(2)}) %all-to-all-start.5) | async-done | bytes 983072 | tf_op jit(solution)/shard_map/all_to_all | solution.py:141
  566.3 4.2 all-to-all-start.6
  573.4 4.2 reshape.368
  577.6 6.7 copy.116
  586.9 4.2 reshape.372
  591.1 6.7 copy.114
  600.4 4.2 reshape.370
  604.6 6.7 copy.115
  614.1 5.4 copy.109
  619.5 7.9 reshape.353
  627.4 8.0 fusion.77
  635.6 12.0 fusion.69
  648.4 10.3 fusion.67
  659.4 6.2 multiply_reduce_fusion.2
  671.9 88.5 %reduce-scatter.8.cloned.1.call-done = f32[192,2304]{1,0:T(8,128)} async-done(((f32[768,2304]{1,0:T(8,128)}), f32[192,2304]{1,0:T(8,128)}) %reduce-scatter.8.cloned.1.call-update) | async-done | bytes 1769488 | tf_op jit(solution)/shard_map/reduce_scatter | solution.py:161
  760.4 164.1 %reduce-scatter.14.cloned.1.call-done = f32[768,768]{1,0:T(8,128)} async-done(((f32[3072,768]{1,0:T(8,128)}), f32[768,768]{1,0:T(8,128)}) %reduce-scatter.14.cloned.1.call-update) | async-done | bytes 2359312 | tf_op jit(solution)/shard_map/reduce_scatter | solution.py:165
  924.5 164.4 %reduce-scatter.12.cloned.1.call-done = f32[192,3072]{1,0:T(8,128)} async-done(((f32[768,3072]{1,0:T(8,128)}), f32[192,3072]{1,0:T(8,128)}) %reduce-scatter.12.cloned.1.call-update) | async-done | bytes 2359312 | tf_op jit(solution)/shard_map/reduce_scatter | solution.py:164
  1090.8 10.8 multiply_convert_fusion.3
  1101.6 11.6 all-reduce.4
  1114.6 24.1 %all-reduce.2 = (f32[5,192]{1,0:T(8,128)}, f32[192]{0:T(256)}, f32[192]{0:T(256)}) all-reduce(f32[5,192]{1,0:T(8,128)S(1)} %copy.118, f32[192]{0:T(256)S(1)} %dynamic-slice.1, f32[192]{0:T(256)S(1)} %dynamic-slice.3), channel_id=1, replica_groups=mesh['items'=8,'heads'=4] {'items'}, use_global_device_ids=true, to_apply=%region_16.17 | all-reduce | flops 1344 | bytes 10752 | tf_op jit(solution)/shard_map/psum | solution.py:168
  1138.7 89.6 %all-reduce.7.cloned.1.call-done = (f32[192,2304]{1,0:T(8,128)}, f32[192,768]{1,0:T(8,128)}, f32[192,3072]{1,0:T(8,128)}, f32[768,768]{1,0:T(8,128)}) async-done(((f32[192,2304]{1,0:T(8,128)}, f32[192,768]{1,0:T(8,128)}, f32[192,3072]{1,0:T(8,128)}, f32[768,768]{1,0:T(8,128)}), (f32[192,2304]{1,0:T(8,128)}, f32[192,768]{1,0:T(8,128)}, f32[192,3072]{1,0:T(8,128)}, ...) | async-done | bytes 7077904 | tf_op jit(solution)/shard_map/psum | solution.py:168
  (257 shorter events, 120.7 us)
Async XLA Ops:
  7.2 11.9 copy-start
  10.1 6.6 copy-start.36
  10.3 3.0 copy-start.50
  13.3 5.8 copy-start.40
  13.4 5.7 copy-start.42
  16.6 6.6 copy-start.46
  107.2 31.9 %all-to-all-start = ((bf16[2,320,12,64]{1,0,3,2:T(2,128)(2,1)}), bf16[2,320,12,64]{1,0,3,2:T(2,128)(2,1)}, u32[]{:S(2)}, u32[]{:S(2)}) async-start(bf16[2,320,12,64]{1,0,3,2:T(2,128)(2,1)} %get-tuple-element.265), calls=%async_computation | async-start | bytes 2359296 | tf_op jit(solution)/shard_map/all_to_all | solution.py:93
  140.6 5.8 copy-start.58
  171.5 11.0 copy-start.22
  171.5 11.0 copy-start.23
  171.5 11.0 copy-start.34
  208.1 10.9 copy-start.22
  208.1 10.9 copy-start.23
  208.1 10.9 copy-start.34
  224.7 19.5 %copy-start.53 = (s32[320]{0:T(512)S(1)}, s32[320]{0:T(512)}, u32[]{:S(2)}) copy-start(s32[320]{0:T(512)} %copy-done.52) | copy-start | bytes 3844
  224.7 19.7 %copy-start.57 = (bf16[768]{0:T(1024)(128)(2,1)S(1)}, bf16[768]{0:T(1024)(128)(2,1)}, u32[]{:S(2)}) copy-start(bf16[768]{0:T(1024)(128)(2,1)} %param.20) | copy-start | bytes 4612
  229.0 38.9 %all-to-all-start.3 = ((bf16[4,2,61440]{2,1,0:T(2,128)(2,1)}), bf16[4,2,61440]{2,1,0:T(2,128)(2,1)}, u32[]{:S(2)}, u32[]{:S(2)}) async-start(bf16[4,2,61440]{2,1,0:T(2,128)(2,1)} %reshape.365), calls=%async_computation.3 | async-start | bytes 1966080 | tf_op jit(solution)/shard_map/all_to_all | solution.py:101
  244.3 59.6 %copy-start.38 = (f32[640]{0:T(1024)}, f32[640]{0:T(1024)S(1)}, u32[]{:S(2)}) copy-start(f32[640]{0:T(1024)S(1)} %reshape.356) | copy-start | bytes 7684
  244.3 58.8 %copy-start.30 = (f32[768]{0:T(1024)}, f32[768]{0:T(1024)S(1)}, u32[]{:S(2)}) copy-start(f32[768]{0:T(1024)S(1)} %convert_element_type.94) | copy-start | bytes 9220
  282.3 4.6 copy-start.61
  285.8 17.4 %copy-start.3 = (f32[640,768]{1,0:T(8,128)}, f32[640,768]{1,0:T(8,128)S(1)}, u32[]{:S(2)}) copy-start(f32[640,768]{1,0:T(8,128)S(1)} %get-tuple-element.273) | copy-start | bytes 5898244
  285.8 17.4 %copy-start.28 = (f32[640]{0:T(1024)}, f32[640]{0:T(1024)S(1)}, u32[]{:S(2)}) copy-start(f32[640]{0:T(1024)S(1)} %broadcast_multiply_fusion) | copy-start | bytes 7684
  285.8 13.2 %slice-start = ((s8[4718592]{0:T(1024)(128)(4,1)}), s8[4194304]{0:T(1024)(128)(4,1)S(1)}, s32[]{:S(2)}) async-start(s8[4718592]{0:T(1024)(128)(4,1)} %bitcast.238), calls=%async_computation.19 | async-start | bytes 8388608
  286.9 16.2 %copy-start.32 = (f32[640]{0:T(1024)}, f32[640]{0:T(1024)S(1)}, u32[]{:S(2)}) copy-start(f32[640]{0:T(1024)S(1)} %fusion.65) | copy-start | bytes 7684
  286.9 12.0 slice-start.1
  298.9 4.2 copy-start.13
  303.1 2.1 copy-start.9
  303.9 2.6 copy-start.24
  348.2 5.9 copy-start.59
  358.2 11.7 copy-start.2
  358.2 11.7 copy-start.14
  370.0 9.9 copy-start.8
  379.8 12.8 %copy-start.15 = (bf16[2,1280,3,64]{1,3,2,0:T(8,128)(2,1)}, bf16[2,1280,3,64]{1,3,2,0:T(8,128)(2,1)S(1)}, u32[]{:S(2)}) copy-start(bf16[2,1280,3,64]{1,3,2,0:T(8,128)(2,1)S(1)} %fusion.135) | copy-start | bytes 2949124 | tf_op jit(solution)/shard_map/while
  392.6 13.8 %copy-start.6 = (bf16[2,1280,3,64]{1,3,2,0:T(8,128)(2,1)S(1)}, bf16[2,1280,3,64]{1,3,2,0:T(8,128)(2,1)}, u32[]{:S(2)}) copy-start(bf16[2,1280,3,64]{1,3,2,0:T(8,128)(2,1)} %get-tuple-element.442) | copy-start | bytes 2949124 | tf_op jit(solution)/shard_map/while
  392.6 13.9 %copy-start.16 = (bf16[2,1280,3,64]{1,3,2,0:T(8,128)(2,1)S(1)}, bf16[2,1280,3,64]{1,3,2,0:T(8,128)(2,1)}, u32[]{:S(2)}) copy-start(bf16[2,1280,3,64]{1,3,2,0:T(8,128)(2,1)} %get-tuple-element.427) | copy-start | bytes 2949124 | tf_op jit(solution)/shard_map/while
  406.5 3.1 copy-start.7
  406.5 3.1 copy-start.18
  416.1 11.7 copy-start.2
  416.1 11.7 copy-start.14
  427.8 9.9 copy-start.8
  437.7 12.8 %copy-start.15 = (bf16[2,1280,3,64]{1,3,2,0:T(8,128)(2,1)}, bf16[2,1280,3,64]{1,3,2,0:T(8,128)(2,1)S(1)}, u32[]{:S(2)}) copy-start(bf16[2,1280,3,64]{1,3,2,0:T(8,128)(2,1)S(1)} %fusion.135) | copy-start | bytes 2949124 | tf_op jit(solution)/shard_map/while
  450.4 13.8 %copy-start.6 = (bf16[2,1280,3,64]{1,3,2,0:T(8,128)(2,1)S(1)}, bf16[2,1280,3,64]{1,3,2,0:T(8,128)(2,1)}, u32[]{:S(2)}) copy-start(bf16[2,1280,3,64]{1,3,2,0:T(8,128)(2,1)} %get-tuple-element.442) | copy-start | bytes 2949124 | tf_op jit(solution)/shard_map/while
  450.4 13.9 %copy-start.16 = (bf16[2,1280,3,64]{1,3,2,0:T(8,128)(2,1)S(1)}, bf16[2,1280,3,64]{1,3,2,0:T(8,128)(2,1)}, u32[]{:S(2)}) copy-start(bf16[2,1280,3,64]{1,3,2,0:T(8,128)(2,1)} %get-tuple-element.427) | copy-start | bytes 2949124 | tf_op jit(solution)/shard_map/while
  464.3 3.1 copy-start.7
  464.3 3.1 copy-start.18
  479.7 44.8 %all-to-all-start.7 = ((bf16[4,2,61440]{2,1,0:T(2,128)(2,1)}), bf16[4,2,61440]{2,1,0:T(2,128)(2,1)}, u32[]{:S(2)}, u32[]{:S(2)}) async-start(bf16[4,2,61440]{2,1,0:T(2,128)(2,1)} %reshape.367), calls=%async_computation.7 | async-start | bytes 1966080 | tf_op jit(solution)/shard_map/all_to_all | solution.py:143
  483.9 187.9 %reduce-scatter.10.cloned.1.call-start = ((), (), s32[]{:S(2)}) async-start(), calls=%async_computation.14 | async-start | bytes 2949120 | tf_op jit(solution)/shard_map/reduce_scatter | solution.py:162
  524.5 41.8 %all-to-all-start.5 = ((bf16[4,2,61440]{2,1,0:T(2,128)(2,1)}), bf16[4,2,61440]{2,1,0:T(2,128)(2,1)}, u32[]{:S(2)}, u32[]{:S(2)}) async-start(bf16[4,2,61440]{2,1,0:T(2,128)(2,1)} %reshape.371), calls=%async_computation.5 | async-start | bytes 1966080 | tf_op jit(solution)/shard_map/all_to_all | solution.py:141
  535.7 34.9 %copy-start.37 = (f32[768]{0:T(1024)S(1)}, f32[768]{0:T(1024)}, u32[]{:S(2)}) copy-start(f32[768]{0:T(1024)} %copy-done.36) | copy-start | bytes 9220
  535.7 34.9 %copy-start.41 = (f32[2,320]{1,0:T(2,128)S(1)}, f32[2,320]{1,0:T(2,128)}, u32[]{:S(2)}) copy-start(f32[2,320]{1,0:T(2,128)} %copy-done.40) | copy-start | bytes 7684
  535.7 34.9 %copy-start.54 = (f32[2,320]{1,0:T(2,128)S(1)}, f32[2,320]{1,0:T(2,128)}, u32[]{:S(2)}) copy-start(f32[2,320]{1,0:T(2,128)} %get-tuple-element.266) | copy-start | bytes 7684
  566.3 34.1 %all-to-all-start.6 = ((bf16[4,2,61440]{2,1,0:T(2,128)(2,1)}), bf16[4,2,61440]{2,1,0:T(2,128)(2,1)}, u32[]{:S(2)}, u32[]{:S(2)}) async-start(bf16[4,2,61440]{2,1,0:T(2,128)(2,1)} %reshape.369), calls=%async_computation.6 | async-start | bytes 1966080 | tf_op jit(solution)/shard_map/all_to_all | solution.py:142
  570.5 189.9 %reduce-scatter.8.cloned.1.call-start = ((), (), s32[]{:S(2)}) async-start(), calls=%async_computation.13 | async-start | bytes 8847360 | tf_op jit(solution)/shard_map/reduce_scatter | solution.py:161
  635.4 289.1 %reduce-scatter.14.cloned.1.call-start = ((), (), s32[]{:S(2)}) async-start(), calls=%async_computation.16 | async-start | bytes 11796480 | tf_op jit(solution)/shard_map/reduce_scatter | solution.py:165
  647.7 441.2 %reduce-scatter.12.cloned.1.call-start = ((), (), s32[]{:S(2)}) async-start(), calls=%async_computation.15 | async-start | bytes 11796480 | tf_op jit(solution)/shard_map/reduce_scatter | solution.py:164
  658.7 6.9 copy-start.47
  658.7 454.9 %reduce-scatter.16.cloned.1.call-start = ((), (), s32[]{:S(2)}) async-start(), calls=%async_computation.17 | async-start | bytes 491520
  659.4 6.2 copy-start.1
  671.8 556.6 %all-reduce.7.cloned.1.call-start = ((), (), s32[]{:S(2)}) async-start(), calls=%async_computation.18 | async-start | bytes 14155776 | tf_op jit(solution)/shard_map/psum | solution.py:168
  1090.8 10.8 copy-start.55
  1090.8 10.8 copy-start.56
  1228.4 3.0 copy-start.27
  1228.4 3.8 copy-start.21
  1232.1 2.5 copy-start.20
  (25 other events, 29.3 us)
Sparse Core Ops, SparseCore 0:
  488.1 66.2 reduce-scatter.9
  635.5 124.8 reduce-scatter.7
  762.7 161.6 reduce-scatter.13
  926.7 162.1 reduce-scatter.11
  1091.6 22.0 reduce-scatter.15
  1117.2 111.1 all-reduce.6
where the time goes:
time: 1250 us; the launch traced here: 1240 us
  waiting for transfers between devices  589 us (47%)
  matrix products  215 us (17%)
  local copies, waits for them, and re-layouts  182 us (15%)
  blocking collectives  133 us (11%)
  other arithmetic  72.9 us (6%)
  starting transfers between devices  34.8 us (3%)
  between operations  15.8 us (1%)
    reduce_scatter x1, waiting for transfers between devices, on_device(): lax.psum_scatter(grad_w_up, 'heads', scatter_dimension=0, tiled=True)  164 us
    reduce_scatter x1, waiting for transfers between devices, on_device(): lax.psum_scatter(grad_w_down, 'heads', scatter_dimension=0, tiled=True)  164 us
    psum x1, waiting for transfers between devices, on_device(): lax.psum((shares[0], shares[1], shares[2], shares[3], shares[4], shares[5...  89.6 us
    reduce_scatter x1, waiting for transfers between devices, on_device(): lax.psum_scatter(grad_w_qkv, 'heads', scatter_dimension=0, tiled=True)  88.5 us
    unnamed x116, local copies, waits for them, and re-layouts  51.2 us
    dot_general x4, matrix products, masked_scores(): jnp.einsum('qhd,khd->hqk', queries, keys_in, preferred_element_type=jnp.f...  47.8 us
    all_to_all x1, blocking collectives, on_device(): lax.all_to_all(keys_local, 'heads', split_axis=2, concat_axis=1, tiled=True)  34.8 us
    all_to_all x1, blocking collectives, on_device(): lax.all_to_all(grad_mixed, 'heads', split_axis=2, concat_axis=1, tiled=True)  31.6 us
  transfers between devices with their start and end apart: 11, of which 9 were waited for; matrix products, arithmetic and copies ran while one was open for 12% of the time, Pallas kernels for 0%

commit v1 on v0

v1 whole, which is shorter than its diff:
```python
import jax
import jax.numpy as jnp
from jax import lax
from jax.experimental import pallas as pl
from jax.experimental.pallas import tpu as pltpu
from jax.sharding import PartitionSpec as P

HEADS = 12
HEAD_DIM = 64
PASSES_MAX = 5
TOK_PASS = 256

epsilon = 1e-05
masked_fill = -1e30
BF16 = jnp.bfloat16
F32 = jnp.float32
NT = (((1,), (1,)), ((), ()))
VMEM_LIMIT = 56 * 1024 * 1024


def matmul(left, right):
    return jnp.dot(left, right, preferred_element_type=F32)


def layer_norm(values_in, gain):
    centered = values_in - jnp.mean(values_in, axis=-1, keepdims=True)
    spread = jnp.mean(centered * centered, axis=-1, keepdims=True)
    return centered * lax.rsqrt(spread + epsilon) * gain


def gelu_tanh(values_in):
    return jax.nn.gelu(values_in, approximate=True)


def causal(scores_t, block):
    shape = (block, block)
    allowed = lax.broadcasted_iota(jnp.int32, shape, 0) <= lax.broadcasted_iota(jnp.int32, shape, 1)
    return jnp.where(allowed, scores_t, masked_fill)


def forward_kernel(heads_here, passes, tok, embed, gain, w_here, mixed, normed_out, qkv, lse, vt, ot):
    block = TOK_PASS
    full_len, width = tok.shape
    blocks = full_len // block
    count = passes[pl.program_id(0)]
    inverse = 1.0 / count.astype(F32)
    embed_rows = embed.shape[0]
    inner = heads_here * HEAD_DIM

    def project(index, carry):
        rows = pl.ds(pl.multiple_of(index * block, block), block)
        slot = lax.broadcasted_iota(jnp.int32, (block, embed_rows), 0) + index * block
        turn = jnp.floor((slot.astype(F32) + 0.5) * inverse).astype(jnp.int32)
        pass_index = slot - turn * count
        onehot = (pass_index == lax.broadcasted_iota(jnp.int32, (block, embed_rows), 1)).astype(F32)
        hidden = tok[rows, :].astype(F32) + matmul(onehot.astype(BF16), embed[...])
        normed = layer_norm(hidden, gain[...]).astype(BF16)
        normed_out[rows, :] = normed
        projected = matmul(normed, w_here[...])
        for piece in range(3 * heads_here):
            part = projected[:, piece * HEAD_DIM:(piece + 1) * HEAD_DIM]
            if piece < heads_here:
                part = part.astype(BF16).astype(F32) * HEAD_DIM ** (-0.5)
            qkv[piece, rows, :] = part.astype(BF16)
        vt[index] = projected[:, 2 * inner:].T.astype(BF16)
        return carry

    lax.fori_loop(0, blocks, project, 0)

    for at in range(blocks):
        here = slice(at * block, (at + 1) * block)

        @pl.when(at < count)
        def _():
            def one_head(head, carry):
                query = qkv[head, here, :]
                diagonal = causal(
                    lax.dot_general(qkv[heads_here + head, here, :], query, NT, preferred_element_type=F32), block
                )
                top = jnp.max(diagonal, axis=0, keepdims=True)
                if at:
                    before = lax.dot_general(
                        qkv[heads_here + head, 0:at * block, :], query, NT, preferred_element_type=F32
                    )
                    top = jnp.maximum(top, jnp.max(before, axis=0, keepdims=True))
                weight = jnp.exp(diagonal - top)
                total = jnp.sum(weight, axis=0, keepdims=True)
                head_rows = pl.ds(pl.multiple_of(head * HEAD_DIM, HEAD_DIM), HEAD_DIM)
                out = matmul(vt[at, head_rows, :], weight.astype(BF16))
                if at:
                    weight = jnp.exp(before - top)
                    total = total + jnp.sum(weight, axis=0, keepdims=True)
                    weight = weight.astype(BF16)
                    for key_at in range(at):
                        out = out + matmul(
                            vt[key_at, head_rows, :], weight[key_at * block:(key_at + 1) * block]
                        )
                ot[head_rows, :] = out * (1.0 / total)
                lse[pl.ds(head, 1), here] = top + jnp.log(total)
                return carry

            lax.fori_loop(0, heads_here, one_head, 0)
            mixed[here, :] = ot[...].T.astype(BF16)

        @pl.when(at >= count)
        def _():
            mixed[here, :] = jnp.zeros((block, inner), BF16)


def backward_kernel(heads_here, passes, qkv, lse, grad_mixed, grad_qkv, grad_heads, kt, sums, grads):
    block = TOK_PASS
    full_len = grad_mixed.shape[0]
    blocks = full_len // block
    count = passes[pl.program_id(0)]

    def split(index, carry):
        rows = pl.ds(pl.multiple_of(index * block, block), block)
        for head in range(heads_here):
            grad_heads[head, rows, :] = grad_mixed[rows, head * HEAD_DIM:(head + 1) * HEAD_DIM]
            kt[head, index] = qkv[heads_here + head, rows, :].astype(F32).T.astype(BF16)
        return carry

    lax.fori_loop(0, blocks, split, 0)

    def one_head(head, carry):
        sums[...] = jnp.zeros_like(sums)
        for at in range(blocks):
            here = slice(at * block, (at + 1) * block)

            @pl.when(at < count)
            def _():
                query = qkv[head, here, :]
                grad = grad_heads[head, here, :]
                row_lse = lse[pl.ds(head, 1), here]
                upto = (at + 1) * block
                keys = qkv[heads_here + head, 0:upto, :]
                values = qkv[2 * heads_here + head, 0:upto, :]
                scores = lax.dot_general(keys, query, NT, preferred_element_type=F32)
                pieces = [scores[:at * block]] if at else []
                pieces.append(causal(scores[at * block:], block))
                prob = [jnp.exp(piece - row_lse) for piece in pieces]
                back = lax.dot_general(values, grad, NT, preferred_element_type=F32)
                back = ([back[:at * block]] if at else []) + [back[at * block:]]
                inner = sum(
                    jnp.sum(one * two, axis=0, keepdims=True) for one, two in zip(prob, back)
                )
                bounds = ([(0, at * block)] if at else []) + [(at * block, upto)]
                turned = None
                for (low, high), one, two in zip(bounds, prob, back):
                    shift = (one * (two - inner)).astype(BF16)
                    sums[1, low:high, :] += matmul(one.astype(BF16), grad)
                    sums[0, low:high, :] += matmul(shift, query)
                    for key_at in range(low // block, high // block):
                        part = matmul(
                            kt[head, key_at], shift[key_at * block - low:(key_at + 1) * block - low]
                        )
                        turned = part if turned is None else turned + part
                grads[head, here, :] = (turned * HEAD_DIM ** (-0.5)).T.astype(BF16)

            @pl.when(at >= count)
            def _():
                grads[head, here, :] = jnp.zeros((block, HEAD_DIM), BF16)

        grads[heads_here + head] = sums[0].astype(BF16)
        grads[2 * heads_here + head] = sums[1].astype(BF16)
        return carry

    lax.fori_loop(0, heads_here, one_head, 0)

    def join(index, carry):
        rows = pl.ds(pl.multiple_of(index * block, block), block)
        grad_qkv[rows, :] = jnp.concatenate([grads[piece, rows, :] for piece in range(3 * heads_here)], axis=1)
        return carry

    lax.fori_loop(0, blocks, join, 0)


def attention_forward(tok_all, passes, embed, gain_one, w_here):
    items, full_len, width = tok_all.shape
    inner = w_here.shape[1] // 3
    heads_here = inner // HEAD_DIM
    blocks = full_len // TOK_PASS
    embed_low = jnp.zeros((128, width), BF16).at[:PASSES_MAX].set(embed)

    def whole(*dims):
        return pl.BlockSpec(dims, lambda i, *_: (0,) * len(dims))

    def per_item(*dims):
        return pl.BlockSpec((None, *dims), lambda i, *_: (i,) + (0,) * len(dims))

    return pl.pallas_call(
        lambda *refs: forward_kernel(heads_here, *refs),
        name="attention_forward",
        grid_spec=pltpu.PrefetchScalarGridSpec(
            num_scalar_prefetch=1,
            grid=(items,),
            in_specs=[per_item(full_len, width), whole(128, width), whole(1, width), whole(width, 3 * inner)],
            out_specs=[
                per_item(full_len, inner),
                per_item(full_len, width),
                per_item(3 * heads_here, full_len, HEAD_DIM),
                per_item(8, full_len),
            ],
            scratch_shapes=[
                pltpu.VMEM((blocks, inner, TOK_PASS), BF16),
                pltpu.VMEM((inner, TOK_PASS), F32),
            ],
        ),
        out_shape=[
            jax.ShapeDtypeStruct((items, full_len, inner), BF16),
            jax.ShapeDtypeStruct((items, full_len, width), BF16),
            jax.ShapeDtypeStruct((items, 3 * heads_here, full_len, HEAD_DIM), BF16),
            jax.ShapeDtypeStruct((items, 8, full_len), F32),
        ],
        compiler_params=pltpu.CompilerParams(vmem_limit_bytes=VMEM_LIMIT),
        cost_estimate=pl.CostEstimate(flops=8 * 10**9, bytes_accessed=16 * 10**6, transcendentals=6 * 10**6),
    )(passes, tok_all, embed_low, gain_one.astype(F32)[None], w_here)


def attention_backward(passes, qkv, lse, grad_mixed):
    items, full_len, inner = grad_mixed.shape
    heads_here = inner // HEAD_DIM
    blocks = full_len // TOK_PASS

    def per_item(*dims):
        return pl.BlockSpec((None, *dims), lambda i, *_: (i,) + (0,) * len(dims))

    return pl.pallas_call(
        lambda *refs: backward_kernel(heads_here, *refs),
        name="attention_backward",
        grid_spec=pltpu.PrefetchScalarGridSpec(
            num_scalar_prefetch=1,
            grid=(items,),
            in_specs=[
                per_item(3 * heads_here, full_len, HEAD_DIM),
                per_item(8, full_len),
                per_item(full_len, inner),
            ],
            out_specs=per_item(full_len, 3 * inner),
            scratch_shapes=[
                pltpu.VMEM((heads_here, full_len, HEAD_DIM), BF16),
                pltpu.VMEM((heads_here, blocks, HEAD_DIM, TOK_PASS), BF16),
                pltpu.VMEM((2, full_len, HEAD_DIM), F32),
                pltpu.VMEM((3 * heads_here, full_len, HEAD_DIM), BF16),
            ],
        ),
        out_shape=jax.ShapeDtypeStruct((items, full_len, 3 * inner), BF16),
        compiler_params=pltpu.CompilerParams(vmem_limit_bytes=VMEM_LIMIT),
        cost_estimate=pl.CostEstimate(flops=20 * 10**9, bytes_accessed=16 * 10**6, transcendentals=6 * 10**6),
    )(passes, qkv, lse, grad_mixed)


def reduce_rows(grad):
    low = grad.astype(BF16)
    return low


def on_device(tokens, passes, embed, gain_one, w_qkv, w_out, gain_two, w_up, w_down, cotangent):
    groups = lax.axis_size("heads")
    place = lax.axis_index("heads")
    item_count, span_here, width = tokens.shape
    row_count = item_count * span_here
    full_len = span_here * groups
    inner = width // groups
    slot_index = place * span_here + jnp.arange(span_here, dtype=jnp.int32)
    valid_len = TOK_PASS * passes
    row_mask = (slot_index[None, :] < valid_len[:, None]).astype(F32).reshape(row_count, 1)
    pass_index = (slot_index[None, :] % passes[:, None]).reshape(row_count, 1)
    onehot = (pass_index == jnp.arange(PASSES_MAX, dtype=jnp.int32)[None, :]).astype(BF16)

    tok_all = lax.all_gather(tokens, "heads", axis=1, tiled=True)
    w_here = lax.dynamic_index_in_dim(w_qkv.reshape(width, 3, groups, inner), place, 2, keepdims=False)
    w_here = w_here.reshape(width, 3 * inner)
    head_mixed, normed_all, qkv, lse = attention_forward(tok_all, passes, embed, gain_one, w_here)

    hidden = tokens.astype(F32).reshape(row_count, width) + matmul(onehot, embed)

    def to_slots(full):
        parts = full.reshape(item_count, groups, span_here, inner).transpose(1, 0, 2, 3)
        parts = lax.all_to_all(parts, "heads", split_axis=0, concat_axis=0, tiled=True)
        return parts.reshape(groups, row_count, inner)

    def to_heads(parts):
        parts = lax.all_to_all(
            parts.reshape(groups, item_count, span_here, inner), "heads", split_axis=0, concat_axis=0, tiled=True
        )
        return parts.transpose(1, 0, 2, 3).reshape(item_count, full_len, inner)

    mixed_rows = to_slots(head_mixed).transpose(1, 0, 2).reshape(row_count, width)
    middle = hidden + matmul(mixed_rows, w_out)
    second, norm_two_back = jax.vjp(layer_norm, middle, gain_two.astype(F32))
    second_low = second.astype(BF16)
    up_proj = matmul(second_low, w_up)
    active, gelu_back = jax.vjp(gelu_tanh, up_proj)
    active_low = active.astype(BF16)
    result = middle + matmul(active_low, w_down)
    outputs = (result * row_mask).astype(BF16).reshape(item_count, span_here, width)
    grad_result = cotangent.astype(F32).reshape(row_count, width) * row_mask
    grad_low = grad_result.astype(BF16)
    (grad_up,) = gelu_back(matmul(grad_low, w_down.T))
    grad_up_low = grad_up.astype(BF16)
    grad_middle_norm, grad_gain_two = norm_two_back(matmul(grad_up_low, w_up.T))
    grad_middle = grad_result + grad_middle_norm
    grad_branch = grad_middle.astype(BF16)
    grad_mixed = matmul(grad_branch, w_out.T).astype(BF16)
    head_grad = to_heads(grad_mixed.reshape(row_count, groups, inner).transpose(1, 0, 2))

    grad_w_down = matmul(active_low.T, grad_low).astype(BF16)
    grad_w_up = matmul(second_low.T, grad_up_low).astype(BF16)
    grad_w_out = matmul(mixed_rows.T, grad_branch).astype(BF16)

    def over_items(grad):
        return lax.psum_scatter(
            grad.reshape(groups, -1, *grad.shape[1:]), "items", scatter_dimension=1, tiled=True
        )

    head_grad, grad_w_down, grad_w_up, grad_w_out = lax.optimization_barrier(
        (head_grad, grad_w_down, grad_w_up, grad_w_out)
    )
    share_down = over_items(grad_w_down)
    share_up = over_items(grad_w_up)
    share_out = over_items(grad_w_out)

    grad_here = attention_backward(passes, qkv, lse, head_grad)
    flat_here = grad_here.reshape(item_count * full_len, 3 * inner)
    partial_norm = matmul(flat_here, w_here.T).astype(BF16).reshape(item_count, full_len, width)
    back_norm = lax.psum_scatter(partial_norm, "heads", scatter_dimension=1, tiled=True)
    grad_w_here = matmul(normed_all.reshape(item_count * full_len, width).T, flat_here).astype(BF16)
    share_qkv = over_items(grad_w_here)

    def finish(share):
        share = lax.psum_scatter(share, "heads", scatter_dimension=0, tiled=True)[0]
        return lax.all_gather(share, "items", axis=0, tiled=True).astype(F32)

    down_total, up_total, out_total = finish(share_down), finish(share_up), finish(share_out)
    share_qkv = lax.all_to_all(share_qkv, "heads", split_axis=0, concat_axis=0, tiled=True)
    qkv_total = lax.all_gather(share_qkv, "items", axis=1, tiled=True)
    qkv_total = qkv_total.reshape(groups, inner, 3, inner).transpose(1, 2, 0, 3).reshape(inner, 3 * width)
    qkv_total = qkv_total.astype(F32)

    _, norm_one_back = jax.vjp(layer_norm, hidden, gain_one.astype(F32))
    grad_hidden_norm, grad_gain_one = norm_one_back(back_norm.reshape(row_count, width).astype(F32))
    grad_hidden = grad_middle + grad_hidden_norm
    grad_tokens = grad_hidden.astype(BF16).reshape(item_count, span_here, width)
    grad_embed = lax.dot_general(
        onehot.astype(F32), grad_hidden, (((0,), (0,)), ((), ())), precision=lax.Precision.HIGHEST
    )
    small = jnp.concatenate([grad_embed, grad_gain_one[None], grad_gain_two[None]], axis=0)
    small = lax.psum(small, ("items", "heads"))
    small = lax.dynamic_slice_in_dim(small, place * inner, inner, axis=1)
    return (
        outputs,
        grad_tokens,
        small[:PASSES_MAX],
        small[PASSES_MAX],
        qkv_total,
        out_total,
        small[PASSES_MAX + 1],
        up_total,
        down_total,
    )


def solution(mesh):
    return jax.shard_map(
        on_device,
        mesh=mesh,
        in_specs=(
            P("items", "heads", None),
            P("items"),
            P(),
            P(),
            P(),
            P(),
            P(),
            P(),
            P(),
            P("items", "heads", None),
        ),
        out_specs=(
            P("items", "heads", None),
            P("items", "heads", None),
            P(None, "heads"),
            P("heads"),
            P("heads", None),
            P("heads", None),
            P("heads"),
            P("heads", None),
            P("heads", None),
        ),
        check_vma=False,
    )
```

time: 1250 us -> 620 us (0.50)
  waiting for transfers between devices: 589 us -> 325 us
  matrix products: 215 us -> 74.3 us
  local copies, waits for them, and re-layouts: 182 us -> 66.1 us
  blocking collectives: 133 us -> 59.6 us
  other arithmetic: 72.9 us -> 17.3 us
  Pallas kernels: 0 us -> 42.5 us
  starting transfers between devices: 34.8 us -> 15.7 us
    reduce_scatter x4 -> x5, waiting for transfers between devices: 417 us -> 110 us  [the longest x1 48.3 us: on_device(): lax.psum_scatter(partial_norm, 'heads', scatter_dimension=1, tiled=True)]
    dot_general x28 -> x13, matrix products: 215 us -> 74.3 us  [the longest x12 73.4 us: matmul(): return jnp.dot(left, right, preferred_element_type=F32)]
    unnamed x7 -> x14, waiting for transfers between devices: 0.36 us -> 125 us
    all_to_all x3 -> x0, blocking collectives: 97.3 us -> none  [the longest x1 34.8 us: on_device(): lax.all_to_all(keys_local, 'heads', split_axis=2, concat_axis=1, tiled=True)]
    psum x1 -> x0, waiting for transfers between devices: 89.6 us -> none  [on_device(): lax.psum((shares[0], shares[1], shares[2], shares[3], shares[4], shares[5...]
    all_gather x0 -> x3, waiting for transfers between devices: none -> 70.2 us  [the longest x1 67.8 us: on_device(): tok_all = lax.all_gather(tokens, 'heads', axis=1, tiled=True)]
    all_to_all x5 -> x3, waiting for transfers between devices: 81.7 us -> 19.9 us  [the longest x1 12.7 us: to_slots(): lax.all_to_all(parts, 'heads', split_axis=0, concat_axis=0, tiled=True)]
    all_to_all x19 -> x1, local copies, waits for them, and re-layouts: 57.2 us -> 0.05 us  [on_device(): lax.all_to_all(share_qkv, 'heads', split_axis=0, concat_axis=0, tiled=True)]
  transfers between devices with their start and end apart: 11 -> 14, of which waited for: 9 -> 11; matrix products, arithmetic and copies ran while one was open for 12% -> 19% of each run, Pallas kernels for 0% -> 3%
where the time goes in v1:
time: 620 us; the launch traced here: 615 us
  waiting for transfers between devices  325 us (52%)
  matrix products  74.3 us (12%)
  local copies, waits for them, and re-layouts  66.1 us (11%)
  blocking collectives  59.6 us (10%)
  Pallas kernels  42.5 us (7%)
  other arithmetic  17.3 us (3%)
  starting transfers between devices  15.7 us (3%)
  between operations  14.7 us (2%)
    unnamed x14, waiting for transfers between devices  125 us
    dot_general x12, matrix products, matmul(): return jnp.dot(left, right, preferred_element_type=F32)  73.4 us
    all_gather x1, waiting for transfers between devices, on_device(): tok_all = lax.all_gather(tokens, 'heads', axis=1, tiled=True)  67.8 us
    reduce_scatter x1, waiting for transfers between devices, on_device(): lax.psum_scatter(partial_norm, 'heads', scatter_dimension=1, tiled=True)  48.3 us
    reduce_scatter x3, waiting for transfers between devices, finish(): share = lax.psum_scatter(share, 'heads', scatter_dimension=0, tiled=True)[0]  42.2 us
    psum x1, blocking collectives, on_device(): small = lax.psum(small, ('items', 'heads'))  38.8 us
    unnamed x61, local copies, waits for them, and re-layouts  33.8 us
    pallas_call x1, Pallas kernels, attention_forward(): pl.pallas_call(lambda *refs: forward_kernel(heads_here, *refs), name='att...  23 us
  transfers between devices with their start and end apart: 14, of which 11 were waited for; matrix products, arithmetic and copies ran while one was open for 19% of the time, Pallas kernels for 3%

profile of v1, /device:TPU:0, one launch (start us, length us, event | category | flops | bytes accessed | tf_op | source)
XLA Modules:
  0.0 615.2 jit_solution(13706982641934740076)
XLA Ops:
  9.8 1.3 broadcast_in_dim.10.refs_3_
  11.8 5.7 copy.56
  17.5 1.3 constant_dynamic-slice_fusion.1
  18.8 1.3 copy.57.refs_4_
  20.9 67.8 %all-gather.7.cloned.1.call-done.refs_1_ = bf16[2,1280,768]{2,1,0:T(8,128)(2,1)} async-done(((bf16[2,320,768]{2,1,0:T(8,128)(2,1)}), bf16[2,1280,768]{2,1,0:T(8,128)(2,1)}) %all-gather.7.cloned.1.call-update) | async-done | bytes 3932176 | tf_op jit(solution)/shard_map/all_gather | solution.py:271
  88.7 23.0 %attention_forward.1 = (bf16[2,1280,192]{2,1,0:T(8,128)(2,1)}, bf16[2,1280,768]{2,1,0:T(8,128)(2,1)}, bf16[2,9,1280,64]{3,2,1,0:T(8,128)(2,1)}, f32[2,8,1280]{2,1,0:T(8,128)}) custom-call(s32[2]{0:T(128)} %refs_0_.3, bf16[2,1280,768]{2,1,0:T(8,128)(2,1)} %all-gather.7.cloned.1.call-done.refs_1_, bf16[128,768]{1,0:T(8,128)(2,1)} %scatter.4.refs_2_, ...), custom_call_target="tpu_custom_call" | custom-call | flops 8000000000 | bytes 16000000 | tf_op jit(solution)/shard_map/attention_forward/pallas_call | solution.py:191
  111.8 3.9 copy.58
  115.6 4.5 all-to-all-start
  120.4 0.9 copy-done.9
  121.9 7.7 %fusion.26 = f32[640,3072]{1,0:T(8,128)} fusion(bf16[640,768]{1,0:T(8,128)(2,1)S(1)} %fusion.12, bf16[3072,768]{1,0:T(8,128)(2,1)} %param.20), kind=kOutput, calls=%fused_computation.72 | convolution fusion | flops 3019898880 | bytes 13565952 | tf_op jit(solution)/shard_map/dot_general | solution.py:22
  129.6 12.7 %all-to-all-done = bf16[4,2,320,192]{2,1,3,0:T(2,128)(2,1)} async-done(((bf16[4,2,320,192]{2,1,3,0:T(2,128)(2,1)}), bf16[4,2,320,192]{2,1,3,0:T(2,128)(2,1)}, u32[]{:S(2)}, u32[]{:S(2)}) %all-to-all-start) | async-done | bytes 983072 | tf_op jit(solution)/shard_map/all_to_all | solution.py:280
  142.2 3.6 reshape.237
  145.8 2.4 fusion.24
  148.6 0.9 copy-done.19
  149.5 12.0 %fusion.6 = (bf16[640,3072]{1,0:T(8,128)(2,1)S(1)}, f32[640,3072]{1,0:T(8,128)}) fusion(f32[640,3072]{1,0:T(8,128)S(1)} %copy-done.19, bf16[768,3072]{1,0:T(8,128)(2,1)} %param.19, f32[640,768]{1,0:T(8,128)S(1)} %get-tuple-element.54, f32[768]{0:T(1024)S(1)} %convert_element_type.85, f32[640]{0:T(1024)S(1)} %fusion.17, f32[640]{0:T(1024)S(1)} %broadcast_multiply_fusion.1), kind=kOutput, calls=%fused_computation.8 | convolution fusion | flops 3061186560 | bytes 26353664 | tf_op jit(solution)/shard_map/dot_general | solution.py:22
  161.5 3.6 multiply_reduce_fusion
  167.2 0.9 copy-done.15
  168.2 1.9 convolution_convert_fusion.4
  170.1 2.0 copy.59
  172.1 1.8 reshape.243
  173.9 5.9 all-to-all-start.1
  179.8 9.0 %convolution_convert_fusion = bf16[768,3072]{1,0:T(8,128)(2,1)} fusion(bf16[640,3072]{1,0:T(8,128)(2,1)} %copy-done.21, f32[640,768]{1,0:T(8,128)} %copy-done.4, f32[768]{0:T(1024)S(1)} %convert_element_type.85, f32[640]{0:T(1024)S(1)} %fusion.17, f32[640]{0:T(1024)S(1)} %broadcast_multiply_fusion.1), kind=kOutput, calls=%fused_computation.10 | convolution fusion | flops 3024224256 | bytes 10625024 | tf_op jit(solution)/shard_map/dot_general | solution.py:22
  188.8 2.1 convolution_convert_fusion.3
  190.9 10.4 %convolution_convert_fusion.1 = bf16[3072,768]{1,0:T(8,128)(2,1)} fusion(bf16[640,768]{1,0:T(8,128)(2,1)S(1)} %copy-done.14, f32[640,3072]{1,0:T(8,128)} %get-tuple-element.56), kind=kOutput, calls=%fused_computation.11 | convolution fusion | flops 3039952896 | bytes 13565952 | tf_op jit(solution)/shard_map/dot_general | solution.py:22
  201.3 7.2 %all-to-all-done.1 = bf16[4,2,320,192]{2,1,3,0:T(2,128)(2,1)S(1)} async-done(((bf16[4,2,320,192]{2,1,3,0:T(2,128)(2,1)}), bf16[4,2,320,192]{2,1,3,0:T(2,128)(2,1)S(1)}, u32[]{:S(2)}, u32[]{:S(2)}) %all-to-all-start.1) | async-done | bytes 983072 | tf_op jit(solution)/shard_map/all_to_all | solution.py:284
  208.5 2.3 copy.60
  210.9 2.2 copy.69
  213.0 1.2 copy.73
  214.5 6.0 copy.71
  220.5 4.0 copy.74
  224.5 19.5 %attention_backward.1 = bf16[2,1280,576]{2,1,0:T(8,128)(2,1)} custom-call(s32[2]{0:T(128)} %refs_0_.3, bf16[2,9,1280,64]{3,2,1,0:T(8,128)(2,1)} %get-tuple-element.30.refs_1_, f32[2,8,1280]{2,1,0:T(8,128)} %get-tuple-element.31.refs_2_, bf16[2,1280,192]{2,1,0:T(8,128)(2,1)} %bitcast.111), custom_call_target="tpu_custom_call" | custom-call | flops 20000000000 | bytes 16000000 | tf_op jit(solution)/shard_map/attention_backward/pallas_call | solution.py:228
  244.0 5.9 bitcast_convert_fusion
  249.8 1.5 copy.62
  251.4 1.7 copy.76
  253.1 2.9 reshape.268
  256.0 19.6 %reduce-scatter.21.cloned.1.call-done = bf16[4,96,768]{2,1,0:T(8,128)(2,1)} async-done(((bf16[4,768,768]{2,1,0:T(8,128)(2,1)}), bf16[4,96,768]{2,1,0:T(8,128)(2,1)}) %reduce-scatter.21.cloned.1.call-update) | async-done | bytes 589840 | tf_op jit(solution)/shard_map/reduce_scatter | solution.py:313
  275.7 40.5 %reduce-scatter.27.cloned.1.call-done = bf16[24,3072]{1,0:T(8,128)(2,1)} async-done(((bf16[192,3072]{1,0:T(8,128)(2,1)}), bf16[24,3072]{1,0:T(8,128)(2,1)}) %reduce-scatter.27.cloned.1.call-update) | async-done | bytes 147472
  316.2 1.0 reshape.271
  318.1 7.1 %convolution_convert_fusion.2 = bf16[2560,768]{1,0:T(8,128)(2,1)} fusion(bf16[2560,576]{1,0:T(8,128)(2,1)} %bitcast.121, bf16[768,576]{0,1:T(8,128)(2,1)S(1)} %bitcast.109), kind=kOutput, calls=%fused_computation.12 | convolution fusion | flops 2266890240 | bytes 7766016 | tf_op jit(solution)/shard_map/dot_general | solution.py:22
  325.3 48.0 %reduce-scatter.29.cloned.1.call-done = bf16[24,12288]{1,0:T(8,128)(2,1)} async-done(((bf16[192,12288]{1,0:T(8,128)(2,1)}), bf16[24,12288]{1,0:T(8,128)(2,1)}) %reduce-scatter.29.cloned.1.call-update) | async-done | bytes 589840
  373.3 1.5 reshape.273
  374.8 1.0 copy.72
  375.9 35.7 %reduce-scatter.25.cloned.1.call-done = bf16[24,2304]{1,0:T(8,128)(2,1)} async-done(((bf16[192,2304]{1,0:T(8,128)(2,1)}), bf16[24,2304]{1,0:T(8,128)(2,1)}) %reduce-scatter.25.cloned.1.call-update) | async-done | bytes 110608
  411.6 1.1 reshape.269
  413.3 4.6 all-to-all-start.2
  417.9 18.6 %reduce-scatter.23.cloned.1.call-done = bf16[1,96,768]{2,1,0:T(8,128)(2,1)} async-done(((bf16[4,96,768]{2,1,0:T(8,128)(2,1)}), bf16[1,96,768]{2,1,0:T(8,128)(2,1)}) %reduce-scatter.23.cloned.1.call-update) | async-done | bytes 147472 | tf_op jit(solution)/shard_map/reduce_scatter | solution.py:332
  436.6 10.8 %multiply_convert_fusion.1 = bf16[640,768]{1,0:T(8,128)(2,1)} fusion(f32[640,768]{1,0:T(8,128)} %copy-done.4, bf16[3072,768]{1,0:T(8,128)(2,1)} %param.20, f32[640]{0:T(1024)S(1)} %compare_convert_fusion, f32[640,3072]{1,0:T(8,128)} %get-tuple-element.56), kind=kOutput, calls=%fused_computation.30 | convolution fusion | flops 3039068160 | bytes 15534592 | tf_op jit(solution)/shard_map/dot_general | solution.py:22
  447.5 11.7 %all_gather.16 = bf16[4,192,576]{2,0,1:T(4,128)(2,1)} all-gather(bf16[4,24,576]{2,0,1:T(4,128)(2,1)S(1)} %copy.63), channel_id=1, replica_groups=mesh['items'=8,'heads'=4] {'items'}, dimensions={1}, use_global_device_ids=true | all-gather | bytes 995328 | tf_op jit(solution)/shard_map/all_gather | solution.py:337
  459.2 2.5 copy.64
  461.8 1.6 convert_bitcast_fusion
  463.4 4.5 copy.65
  467.9 3.7 reshape.259
  471.6 9.1 %all-gather = bf16[1,192,768]{2,1,0:T(8,128)(2,1)S(1)} all-gather(bf16[1,24,768]{2,1,0:T(8,128)(2,1)} %reduce-scatter.17.cloned.1.call-done), channel_id=2, replica_groups=mesh['items'=8,'heads'=4] {'items'}, dimensions={1}, use_global_device_ids=true | all-gather | bytes 331776 | tf_op jit(solution)/shard_map/all_gather | solution.py:333
  480.7 0.9 bitcast_convert_fusion.3
  481.5 48.3 %reduce-scatter.15.cloned.1.call-done = bf16[2,320,768]{2,1,0:T(8,128)(2,1)} async-done(((bf16[2,1280,768]{2,1,0:T(8,128)(2,1)}), bf16[2,320,768]{2,1,0:T(8,128)(2,1)}) %reduce-scatter.15.cloned.1.call-update) | async-done | bytes 983056 | tf_op jit(solution)/shard_map/reduce_scatter | solution.py:327
  529.8 1.9 multiply_reduce_fusion.1
  531.7 23.6 %reduce-scatter.19.cloned.1.call-done = bf16[1,24,3072]{2,1,0:T(8,128)(2,1)} async-done(((bf16[4,24,3072]{2,1,0:T(8,128)(2,1)}), bf16[1,24,3072]{2,1,0:T(8,128)(2,1)}) %reduce-scatter.19.cloned.1.call-update) | async-done | bytes 147472 | tf_op jit(solution)/shard_map/reduce_scatter | solution.py:332
  555.4 1.1 fusion.10
  557.1 1.9 fusion.21
  559.0 0.9 fusion.14
  559.9 38.8 %psum.7 = f32[7,768]{1,0:T(8,128)S(1)} all-reduce(f32[7,768]{1,0:T(8,128)S(1)} %pad_maximum_fusion), channel_id=1, replica_groups=mesh['items'=8,'heads'=4] {'items','heads'}, use_global_device_ids=true, to_apply=%region_11.12 | all-reduce | flops 5376 | bytes 43008 | tf_op jit(solution)/shard_map/psum | solution.py:349
  600.0 2.9 bitcast_convert_fusion.1
  603.0 2.4 all-gather.9.cloned.1.call-done
  605.3 2.9 bitcast_convert_fusion.2
  (107 shorter events, 11.7 us)
Async XLA Ops:
  7.2 138.6 %copy-start = (bf16[768,768]{1,0:T(8,128)(2,1)S(1)}, bf16[768,768]{1,0:T(8,128)(2,1)}, u32[]{:S(2)}) copy-start(bf16[768,768]{1,0:T(8,128)(2,1)} %param.17) | copy-start | bytes 3538948
  7.2 81.6 %all-gather.7.cloned.1.call-start = ((), (), s32[]{:S(2)}) async-start(), calls=%async_computation.11 | async-start | bytes 4915200 | tf_op jit(solution)/shard_map/all_gather | solution.py:271
  17.5 2.6 copy-start.17
  18.8 93.0 %copy-start.11 = (bf16[768,3,1,192]{0,3,2,1:T(8,128)(2,1)}, bf16[768,3,1,192]{0,3,2,1:T(8,128)(2,1)S(1)}, u32[]{:S(2)}) copy-start(bf16[768,3,1,192]{0,3,2,1:T(8,128)(2,1)S(1)} %constant_dynamic-slice_fusion.1) | copy-start | bytes 2654212
  111.8 8.4 %copy-start.6 = (bf16[2,320,768]{2,1,0:T(8,128)(2,1)S(1)}, bf16[2,320,768]{2,1,0:T(8,128)(2,1)}, u32[]{:S(2)}) copy-start(bf16[2,320,768]{2,1,0:T(8,128)(2,1)} %param.21) | copy-start | bytes 2949124
  115.6 26.6 %all-to-all-start = ((bf16[4,2,320,192]{2,1,3,0:T(2,128)(2,1)}), bf16[4,2,320,192]{2,1,3,0:T(2,128)(2,1)}, u32[]{:S(2)}, u32[]{:S(2)}) async-start(bf16[4,2,320,192]{2,1,3,0:T(2,128)(2,1)} %bitcast.99), calls=%async_computation | async-start | bytes 2359296 | tf_op jit(solution)/shard_map/all_to_all | solution.py:280
  120.1 1.2 copy-start.9
  120.4 1.5 copy-start.13
  145.8 3.7 copy-start.19
  148.2 16.9 %copy-start.4 = (f32[640,768]{1,0:T(8,128)}, f32[640,768]{1,0:T(8,128)S(1)}, u32[]{:S(2)}) copy-start(f32[640,768]{1,0:T(8,128)S(1)} %get-tuple-element.54) | copy-start | bytes 5898244
  148.2 13.3 %slice-start = ((s8[4718592]{0:T(1024)(128)(4,1)}), s8[4194304]{0:T(1024)(128)(4,1)S(1)}, s32[]{:S(2)}) async-start(s8[4718592]{0:T(1024)(128)(4,1)} %bitcast.119), calls=%async_computation.22 | async-start | bytes 8388608
  149.5 12.0 %slice-start.1 = ((s8[4718592]{0:T(1024)(128)(4,1)}), s8[524288]{0:T(1024)(128)(4,1)S(1)}, s32[]{:S(2)}) async-start(s8[4718592]{0:T(1024)(128)(4,1)} %bitcast.119), calls=%async_computation.23 | async-start | bytes 1048576
  161.5 3.6 copy-start.21
  165.2 1.2 copy-start.7
  165.9 1.3 copy-start.2
  167.2 0.9 copy-start.15
  173.9 34.6 %all-to-all-start.1 = ((bf16[4,2,320,192]{2,1,3,0:T(2,128)(2,1)}), bf16[4,2,320,192]{2,1,3,0:T(2,128)(2,1)S(1)}, u32[]{:S(2)}, u32[]{:S(2)}) async-start(bf16[4,2,320,192]{2,1,3,0:T(2,128)(2,1)} %reshape.243), calls=%async_computation.1 | async-start | bytes 2359296 | tf_op jit(solution)/shard_map/all_to_all | solution.py:284
  179.8 95.9 %reduce-scatter.21.cloned.1.call-start = ((), (), s32[]{:S(2)}) async-start(), calls=%async_computation.15 | async-start | bytes 5308416 | tf_op jit(solution)/shard_map/reduce_scatter | solution.py:313
  179.8 9.0 %copy-start.10 = (bf16[4,640,192]{1,2,0:T(8,128)(2,1)S(1)}, bf16[4,640,192]{1,2,0:T(8,128)(2,1)}, u32[]{:S(2)}) copy-start(bf16[4,640,192]{1,2,0:T(8,128)(2,1)} %reshape.237) | copy-start | bytes 2949124
  179.8 9.0 %copy-start.16 = (bf16[640,768]{1,0:T(8,128)(2,1)S(1)}, bf16[640,768]{1,0:T(8,128)(2,1)}, u32[]{:S(2)}) copy-start(bf16[640,768]{1,0:T(8,128)(2,1)} %copy-done.15) | copy-start | bytes 2949124
  188.8 2.1 copy-start.14
  210.8 105.4 %reduce-scatter.27.cloned.1.call-start = ((), (), s32[]{:S(2)}) async-start(), calls=%async_computation.20 | async-start | bytes 1327104
  214.3 159.0 %reduce-scatter.29.cloned.1.call-start = ((), (), s32[]{:S(2)}) async-start(), calls=%async_computation.21 | async-start | bytes 5308416
  224.4 187.2 %reduce-scatter.25.cloned.1.call-start = ((), (), s32[]{:S(2)}) async-start(), calls=%async_computation.19 | async-start | bytes 995328
  224.5 19.5 %copy-start.20 = (bf16[2,1280,768]{2,1,0:T(8,128)(2,1)S(1)}, bf16[2,1280,768]{2,1,0:T(8,128)(2,1)}, u32[]{:S(2)}) copy-start(bf16[2,1280,768]{2,1,0:T(8,128)(2,1)} %get-tuple-element.33) | copy-start | bytes 11796484
  253.1 65.1 %copy-start.12 = (bf16[768,3,1,192]{0,3,2,1:T(8,128)(2,1)S(1)}, bf16[768,3,1,192]{0,3,2,1:T(8,128)(2,1)}, u32[]{:S(2)}) copy-start(bf16[768,3,1,192]{0,3,2,1:T(8,128)(2,1)} %copy-done.11) | copy-start | bytes 2654212
  256.0 180.6 %reduce-scatter.23.cloned.1.call-start = ((), (), s32[]{:S(2)}) async-start(), calls=%async_computation.16 | async-start | bytes 737280 | tf_op jit(solution)/shard_map/reduce_scatter | solution.py:332
  275.6 195.9 %reduce-scatter.17.cloned.1.call-start = ((), (), s32[]{:S(2)}) async-start(), calls=%async_computation.13 | async-start | bytes 184320 | tf_op jit(solution)/shard_map/reduce_scatter | solution.py:332
  317.9 211.9 %reduce-scatter.15.cloned.1.call-start = ((), (), s32[]{:S(2)}) async-start(), calls=%async_computation.12 | async-start | bytes 4915200 | tf_op jit(solution)/shard_map/reduce_scatter | solution.py:327
  325.3 50.6 %copy-start.18 = (bf16[768]{0:T(1024)(128)(2,1)S(1)}, bf16[768]{0:T(1024)(128)(2,1)}, u32[]{:S(2)}) copy-start(bf16[768]{0:T(1024)(128)(2,1)} %param.15) | copy-start | bytes 4612
  325.3 230.0 %reduce-scatter.19.cloned.1.call-start = ((), (), s32[]{:S(2)}) async-start(), calls=%async_computation.14 | async-start | bytes 737280 | tf_op jit(solution)/shard_map/reduce_scatter | solution.py:332
  413.3 34.1 %all-to-all-start.2 = ((bf16[4,24,576]{2,1,0:T(8,128)(2,1)}), bf16[4,24,576]{2,1,0:T(8,128)(2,1)S(1)}, u32[]{:S(2)}, u32[]{:S(2)}) async-start(bf16[4,24,576]{2,1,0:T(8,128)(2,1)} %copy.68), calls=%async_computation.3 | async-start | bytes 245760 | tf_op jit(solution)/shard_map/all_to_all | solution.py:336
  417.9 182.1 %all-gather.11.cloned.1.call-start = ((), (), s32[]{:S(2)}) async-start(), calls=%async_computation.18 | async-start | bytes 1327104 | tf_op jit(solution)/shard_map/all_gather | solution.py:333
  436.6 168.8 %all-gather.9.cloned.1.call-start = ((), (), s32[]{:S(2)}) async-start(), calls=%async_computation.17 | async-start | bytes 1327104 | tf_op jit(solution)/shard_map/all_gather | solution.py:333
  529.8 25.6 %copy-start.5 = (bf16[2,320,768]{2,1,0:T(8,128)(2,1)S(1)}, bf16[2,320,768]{2,1,0:T(8,128)(2,1)}, u32[]{:S(2)}) copy-start(bf16[2,320,768]{2,1,0:T(8,128)(2,1)} %reduce-scatter.15.cloned.1.call-done) | copy-start | bytes 2949124
  555.3 1.5 copy-start.3
  555.3 1.8 copy-start.8
  600.0 8.2 %copy-start.1 = (bf16[768,768]{1,0:T(8,128)(2,1)S(1)}, bf16[768,768]{1,0:T(8,128)(2,1)}, u32[]{:S(2)}) copy-start(bf16[768,768]{1,0:T(8,128)(2,1)} %param.17) | copy-start | bytes 3538948
Sparse Core Ops, SparseCore 0:
  9.6 79.1 all-gather.6
  210.9 64.6 reduce-scatter.20
  279.4 36.6 reduce-scatter.26
  319.5 53.7 reduce-scatter.28
  377.0 34.5 reduce-scatter.24
  413.7 22.7 reduce-scatter.22
  439.4 17.2 reduce-scatter.16
  459.0 70.7 reduce-scatter.14
  532.7 22.5 reduce-scatter.18
  557.0 22.4 all-gather.10
  581.4 23.8 all-gather.8
